TPU v7x, 32 devices: a whole 2x2x4 slice. The times are simulated.
32 devices in a mesh: section: 2 (over x), dp: 4 (over z), mp: 4 (over y, core).
Axes of the slice: x: 2, y: 2, z: 4, core: 2. Of those that a mesh axis runs over, the one named last changes fastest.
Arguments:
- text_feats: bfloat16 [4096, 512], P('dp'), may hold values from -48 to 48
- image_feats: bfloat16 [4096, 512], P(('dp', 'mp')), may hold values from -48 to 48
- logit_scale: float32 [1], replicated, may hold values from 10 to 320
- layer_inputs: bfloat16 [2, 4096, 512], P('section', 'dp'), may hold values from -6 to 6
- w_in: bfloat16 [2, 512, 2048], P('section', None, 'mp'), may hold values from -0.25 to 0.25
- w_out: bfloat16 [2, 2048, 512], P('section', 'mp'), may hold values from -0.125 to 0.125
Outputs:
- image_grad: bfloat16 [4096, 512], P(('dp', 'mp'))
- input_grad: bfloat16 [4096, 512], P('dp', 'section')
- w_in_grad: float32 [2, 512, 2048], P('section', 'dp', 'mp')
- w_out_grad_t: float32 [2, 512, 2048], P('section', 'dp', 'mp')
All inputs are finite; a program needn't handle non-finite values.
Results may differ from a plain program's by a relative error of at most 0.017.
Values may be sent and summed in bfloat16 or wider, within the bound.
A program may use at most 128 MiB of HBM per device.

v0:
```python
import jax
import jax.numpy as jnp
from jax import lax
from jax.sharding import PartitionSpec as P

MICRO = 4


def shifted(block, axis, distance):
    devices = range(lax.axis_size(axis))
    route = [(i - distance, i) for i in devices if i - distance in devices]
    return lax.ppermute(block, axis, route)


def spread(value, axis, source):
    kept = jnp.where(lax.axis_index(axis) == source, value, 0).astype(value.dtype)
    return lax.psum(kept, axis)


def unit_rows(values):
    wide = values.astype(jnp.float32)
    length = jnp.sqrt(jnp.sum(wide * wide, axis=1, keepdims=True) + 1.0)
    return (wide / length, length)


def unit_backward(unit, length, grad_unit):
    return (grad_unit - unit * jnp.sum(unit * grad_unit, axis=1, keepdims=True)) / length


def quick_gelu(values):
    return values * jax.nn.sigmoid(1.702 * values)


def quick_slope(values):
    sigm = jax.nn.sigmoid(1.702 * values)
    return sigm + 1.702 * values * sigm * (1.0 - sigm)


def contract_rows(left_side, right_side):
    return lax.dot_general(
        left_side, right_side, (((0,), (0,)), ((), ())), preferred_element_type=jnp.float32
    )


def contract_cols(left_side, right_side):
    return lax.dot_general(
        left_side, right_side, (((1,), (1,)), ((), ())), preferred_element_type=jnp.float32
    )


def body(text_feats, image_feats, logit_scale, layer_inputs, w_in, w_out):
    logit_mult = logit_scale[0]
    mp_count = lax.axis_size("mp")
    segment_count = lax.axis_size("section")
    dp_index = lax.axis_index("dp")
    mp_index = lax.axis_index("mp")
    segment_index = lax.axis_index("section")
    row_count = text_feats.shape[0]
    own_rows = image_feats.shape[0]
    text_unit, text_length = unit_rows(text_feats)
    image_unit, image_length = unit_rows(image_feats)
    text_low = text_unit.astype(jnp.bfloat16)
    image_low = image_unit.astype(jnp.bfloat16)
    columns = lax.all_gather(image_low, "dp", axis=0, tiled=True)
    column_total_count = columns.shape[0]
    scores = logit_mult * contract_cols(text_low, columns)
    text_ids = dp_index * row_count + jnp.arange(row_count, dtype=jnp.int32)
    column_pos = jnp.arange(column_total_count, dtype=jnp.int32)
    image_ids = (column_pos // own_rows * mp_count + mp_index) * own_rows + column_pos % own_rows
    positive = (text_ids[:, None] == image_ids[None, :]).astype(jnp.float32)
    row_peak = lax.pmax(jnp.max(scores, axis=1), "mp")
    column_peak = lax.pmax(jnp.max(scores, axis=0), "dp")
    row_total = lax.psum(jnp.sum(jnp.exp(scores - row_peak[:, None]), axis=1), "mp")
    column_local = jnp.sum(jnp.exp(scores - column_peak[None, :]), axis=0)
    column_total = lax.psum(column_local, "dp")
    row_prob = jnp.exp(scores - row_peak[:, None]) / row_total[:, None]
    column_prob = jnp.exp(scores - column_peak[None, :]) / column_total[None, :]
    score_grad = (0.5 * (row_prob + column_prob) - positive).astype(jnp.bfloat16)
    text_share = logit_mult * jnp.dot(score_grad, columns, preferred_element_type=jnp.float32)
    text_unit_grad = lax.psum(text_share, "mp")
    top_grad = unit_backward(text_unit, text_length, text_unit_grad).astype(jnp.bfloat16)
    image_unit_grad = lax.psum_scatter(
        (logit_mult * contract_rows(score_grad, text_low)).astype(jnp.bfloat16),
        "dp",
        scatter_dimension=0,
        tiled=True,
    ).astype(jnp.float32)
    image_grad = unit_backward(image_unit, image_length, image_unit_grad).astype(jnp.bfloat16)
    segment_inputs = layer_inputs[0]
    w_first = w_in[0]
    w_second = w_out[0]
    step_rows = row_count // MICRO
    last_segment = segment_count - 1
    time_steps = MICRO + segment_count - 1
    is_last = segment_index == last_segment
    is_first = segment_index == 0
    incoming = jnp.zeros((step_rows, segment_inputs.shape[1]), jnp.bfloat16)
    grad_first = jnp.zeros(w_first.shape, jnp.float32)
    grad_second = jnp.zeros(w_first.shape, jnp.float32)
    finished = jnp.zeros((row_count, segment_inputs.shape[1]), jnp.bfloat16)
    for time_step in range(time_steps):
        micro_slot = time_step - last_segment + segment_index
        active = jnp.logical_and(micro_slot >= 0, micro_slot < MICRO)
        row_start = jnp.clip(micro_slot, 0, MICRO - 1) * step_rows
        top_start = min(time_step, MICRO - 1) * step_rows
        top_piece = top_grad[top_start : top_start + step_rows]
        grad_now = jnp.where(is_last, top_piece, incoming)
        inputs_now = lax.dynamic_slice_in_dim(segment_inputs, row_start, step_rows, 0)
        pre_act = jnp.dot(inputs_now, w_first, preferred_element_type=jnp.float32)
        activation = quick_gelu(pre_act).astype(jnp.bfloat16)
        back_grad = contract_cols(grad_now, w_second)
        pre_grad = (back_grad * quick_slope(pre_act)).astype(jnp.bfloat16)
        unit_share = contract_cols(pre_grad, w_first)
        summed = lax.psum(unit_share.astype(jnp.bfloat16), "mp").astype(jnp.float32)
        grad_prev = (grad_now.astype(jnp.float32) + summed).astype(jnp.bfloat16)
        weight = active.astype(jnp.float32)
        grad_first = grad_first + weight * contract_rows(inputs_now, pre_grad)
        grad_second = grad_second + weight * contract_rows(grad_now, activation)
        updated = lax.dynamic_update_slice_in_dim(finished, grad_prev, row_start, 0)
        finished = jnp.where(jnp.logical_and(active, is_first), updated, finished)
        if time_step + 1 < time_steps:
            incoming = shifted(grad_prev, "section", -1)
    whole_grad = spread(finished, "section", 0)
    feature_width = whole_grad.shape[1] // segment_count
    feature_start = segment_index * feature_width
    input_grad = lax.dynamic_slice_in_dim(whole_grad, feature_start, feature_width, 1)
    first_sum, second_sum = (
        lax.psum_scatter(
            grad_first.astype(jnp.bfloat16), "dp", scatter_dimension=0, tiled=True
        ).astype(jnp.float32),
        lax.psum_scatter(
            grad_second.astype(jnp.bfloat16), "dp", scatter_dimension=0, tiled=True
        ).astype(jnp.float32),
    )
    return (image_grad, input_grad, first_sum[None], second_sum[None])


def solution(mesh):
    placed = (
        P("dp", None),
        P(("dp", "mp"), None),
        P(),
        P("section", "dp", None),
        P("section", None, "mp"),
        P("section", "mp", None),
    )
    return jax.shard_map(
        body,
        mesh=mesh,
        in_specs=placed,
        out_specs=(
            P(("dp", "mp"), None),
            P("dp", "section"),
            P("section", "dp", "mp"),
            P("section", "dp", "mp"),
        ),
        check_vma=False,
    )
```

profile of v0, /device:TPU:0, one launch (start us, length us, event | category | flops | bytes accessed | tf_op | source)
XLA Modules:
  0.0 491.8 jit_solution(6473197469235849443)
XLA Ops:
  12.5 28.6 %all-gather.2.cloned.1.call-done = bf16[1024,512]{1,0:T(8,128)(2,1)} async-done(((bf16[256,512]{1,0:T(8,128)(2,1)}), bf16[1024,512]{1,0:T(8,128)(2,1)}) %all-gather.2.cloned.1.call-update) | async-done | bytes 1048592 | tf_op jit(solution)/shard_map/all_gather | solution.py:64
  41.1 4.5 multiply_reduce_fusion.1
  45.7 6.0 %pmax.14 = f32[1024]{0:T(1024)S(1)} all-reduce(f32[1024]{0:T(1024)S(1)} %get-tuple-element.14), channel_id=1, replica_groups=mesh['section'=2,'dp'=4,'mp'=4] {'mp'}, use_global_device_ids=true, to_apply=%region_3.4 | all-reduce | flops 1024 | bytes 8192 | tf_op jit(solution)/shard_map/pmax | solution.py:71
  51.7 3.2 fusion
  54.9 10.9 %pmax.15 = f32[1024]{0:T(1024)S(1)} all-reduce(f32[1024]{0:T(1024)S(1)} %get-tuple-element.5), channel_id=1, replica_groups=mesh['section'=2,'dp'=4,'mp'=4] {'dp'}, use_global_device_ids=true, to_apply=%region_7.8 | all-reduce | flops 1024 | bytes 8192 | tf_op jit(solution)/shard_map/pmax | solution.py:72
  65.8 2.9 fusion.1
  68.7 8.4 %psum.64 = f32[1024]{0:T(1024)S(1)} all-reduce(f32[1024]{0:T(1024)S(1)} %fusion.1), channel_id=1, replica_groups=mesh['section'=2,'dp'=4,'mp'=4] {'dp'}, use_global_device_ids=true, to_apply=%region_9.10 | all-reduce | flops 1024 | bytes 8192 | tf_op jit(solution)/shard_map/psum | solution.py:75
  77.1 5.7 %psum.63 = f32[1024]{0:T(1024)S(1)} all-reduce(f32[1024]{0:T(1024)S(1)} %get-tuple-element.4), channel_id=1, replica_groups=mesh['section'=2,'dp'=4,'mp'=4] {'mp'}, use_global_device_ids=true, to_apply=%region_5.6 | all-reduce | flops 1024 | bytes 8192 | tf_op jit(solution)/shard_map/psum | solution.py:73
  82.8 3.9 subtract_convert_fusion
  92.0 49.2 %all-reduce.8.cloned.1.call-done = f32[1024,512]{1,0:T(8,128)} async-done(((f32[1024,512]{1,0:T(8,128)}), f32[1024,512]{1,0:T(8,128)}) %all-reduce.8.cloned.1.call-update) | async-done | bytes 2097168 | tf_op jit(solution)/shard_map/psum | solution.py:80
  147.1 32.5 %all-reduce.10.cloned.1.call-done = bf16[256,512]{1,0:T(8,128)(2,1)} async-done(((bf16[256,512]{1,0:T(8,128)(2,1)}), bf16[256,512]{1,0:T(8,128)(2,1)}) %all-reduce.10.cloned.1.call-update) | async-done | bytes 262160 | tf_op jit(solution)/shard_map/psum | solution.py:114
  184.0 6.8 %collective-permute-done = bf16[256,512]{1,0:T(8,128)(2,1)S(1)} collective-permute-done((bf16[256,512]{1,0:T(8,128)(2,1)S(1)}, bf16[256,512]{1,0:T(8,128)(2,1)S(1)}, u32[]{:S(2)}, u32[]{:S(2)}) %collective-permute-start) | collective-permute-done | bytes 262176 | tf_op jit(solution)/shard_map/ppermute | solution.py:12
  194.1 32.4 %all-reduce.12.cloned.1.call-done = bf16[256,512]{1,0:T(8,128)(2,1)} async-done(((bf16[256,512]{1,0:T(8,128)(2,1)}), bf16[256,512]{1,0:T(8,128)(2,1)}) %all-reduce.12.cloned.1.call-update) | async-done | bytes 262160 | tf_op jit(solution)/shard_map/psum | solution.py:114
  229.9 6.9 %collective-permute-done.1 = bf16[256,512]{1,0:T(8,128)(2,1)} collective-permute-done((bf16[256,512]{1,0:T(8,128)(2,1)S(1)}, bf16[256,512]{1,0:T(8,128)(2,1)}, u32[]{:S(2)}, u32[]{:S(2)}) %collective-permute-start.1) | collective-permute-done | bytes 262176 | tf_op jit(solution)/shard_map/ppermute | solution.py:12
  241.1 32.4 %all-reduce.14.cloned.1.call-done = bf16[256,512]{1,0:T(8,128)(2,1)} async-done(((bf16[256,512]{1,0:T(8,128)(2,1)}), bf16[256,512]{1,0:T(8,128)(2,1)}) %all-reduce.14.cloned.1.call-update) | async-done | bytes 262160 | tf_op jit(solution)/shard_map/psum | solution.py:114
  277.0 7.1 %collective-permute-done.2 = bf16[256,512]{1,0:T(8,128)(2,1)} collective-permute-done((bf16[256,512]{1,0:T(8,128)(2,1)}, bf16[256,512]{1,0:T(8,128)(2,1)}, u32[]{:S(2)}, u32[]{:S(2)}) %collective-permute-start.2) | collective-permute-done | bytes 262176 | tf_op jit(solution)/shard_map/ppermute | solution.py:12
  288.1 32.4 %all-reduce.16.cloned.1.call-done = bf16[256,512]{1,0:T(8,128)(2,1)} async-done(((bf16[256,512]{1,0:T(8,128)(2,1)}), bf16[256,512]{1,0:T(8,128)(2,1)}) %all-reduce.16.cloned.1.call-update) | async-done | bytes 262160 | tf_op jit(solution)/shard_map/psum | solution.py:114
  324.3 6.9 %collective-permute-done.3 = bf16[256,512]{1,0:T(8,128)(2,1)} collective-permute-done((bf16[256,512]{1,0:T(8,128)(2,1)}, bf16[256,512]{1,0:T(8,128)(2,1)}, u32[]{:S(2)}, u32[]{:S(2)}) %collective-permute-start.3) | collective-permute-done | bytes 262176 | tf_op jit(solution)/shard_map/ppermute | solution.py:12
  335.2 4.0 multiply_convert_fusion
  350.5 17.1 %all-reduce.18.cloned.1.call-done = bf16[256,512]{1,0:T(8,128)(2,1)} async-done(((bf16[256,512]{1,0:T(8,128)(2,1)}), bf16[256,512]{1,0:T(8,128)(2,1)}) %all-reduce.18.cloned.1.call-update) | async-done | bytes 262160 | tf_op jit(solution)/shard_map/psum | solution.py:114
  371.8 25.4 %reduce-scatter.4.cloned.1.call-done = bf16[256,512]{1,0:T(8,128)(2,1)} async-done(((bf16[1024,512]{1,0:T(8,128)(2,1)}), bf16[256,512]{1,0:T(8,128)(2,1)}) %reduce-scatter.4.cloned.1.call-update) | async-done | bytes 262160 | tf_op jit(solution)/shard_map/reduce_scatter | solution.py:82
  400.2 20.2 %reduce-scatter.6.cloned.1.call-done = bf16[128,512]{1,0:T(8,128)(2,1)} async-done(((bf16[512,512]{1,0:T(8,128)(2,1)}), bf16[128,512]{1,0:T(8,128)(2,1)}) %reduce-scatter.6.cloned.1.call-update) | async-done | bytes 131088 | tf_op jit(solution)/shard_map/reduce_scatter | solution.py:128
  422.1 20.6 %reduce-scatter.8.cloned.1.call-done = bf16[128,512]{1,0:T(8,128)(2,1)} async-done(((bf16[512,512]{1,0:T(8,128)(2,1)}), bf16[128,512]{1,0:T(8,128)(2,1)}) %reduce-scatter.8.cloned.1.call-update) | async-done | bytes 131088 | tf_op jit(solution)/shard_map/reduce_scatter | solution.py:131
  444.3 39.1 %all-reduce.20.cloned.1.call-done = bf16[1024,512]{1,0:T(8,128)(2,1)} async-done(((bf16[1024,512]{1,0:T(8,128)(2,1)}), bf16[1024,512]{1,0:T(8,128)(2,1)}) %all-reduce.20.cloned.1.call-update) | async-done | bytes 1048592 | tf_op jit(solution)/shard_map/psum | solution.py:17
  (142 shorter events, 69.7 us)
Async XLA Ops:
  7.2 83.5 %copy-start = (bf16[1,1024,512]{2,1,0:T(8,128)(2,1)S(1)}, bf16[1,1024,512]{2,1,0:T(8,128)(2,1)}, u32[]{:S(2)}) copy-start(bf16[1,1024,512]{2,1,0:T(8,128)(2,1)} %param.9) | copy-start | bytes 3145732
  7.2 34.0 %copy-start.2 = (bf16[1024,512]{1,0:T(8,128)(2,1)S(1)}, bf16[1024,512]{1,0:T(8,128)(2,1)}, u32[]{:S(2)}) copy-start(bf16[1024,512]{1,0:T(8,128)(2,1)} %param.6) | copy-start | bytes 3145732
  7.2 33.9 %all-gather.2.cloned.1.call-start = ((), (), s32[]{:S(2)}) async-start(), calls=%async_computation.3 | async-start | bytes 1310720 | tf_op jit(solution)/shard_map/all_gather | solution.py:64
  10.3 130.9 %all-reduce.8.cloned.1.call-start = ((), (), s32[]{:S(2)}) async-start(), calls=%async_computation.5 | async-start | bytes 4194304 | tf_op jit(solution)/shard_map/psum | solution.py:80
  90.6 88.9 %all-reduce.10.cloned.1.call-start = ((), (), s32[]{:S(2)}) async-start(), calls=%async_computation.6 | async-start | bytes 524288 | tf_op jit(solution)/shard_map/psum | solution.py:114
  92.0 51.9 %copy-start.23 = (f32[256,512]{1,0:T(8,128)}, f32[256,512]{1,0:T(8,128)S(1)}, u32[]{:S(2)}) copy-start(f32[256,512]{1,0:T(8,128)S(1)} %fusion.35) | copy-start | bytes 1572868
  147.0 79.4 %all-reduce.12.cloned.1.call-start = ((), (), s32[]{:S(2)}) async-start(), calls=%async_computation.7 | async-start | bytes 524288 | tf_op jit(solution)/shard_map/psum | solution.py:114
  182.4 8.4 %collective-permute-start = (bf16[256,512]{1,0:T(8,128)(2,1)S(1)}, bf16[256,512]{1,0:T(8,128)(2,1)S(1)}, u32[]{:S(2)}, u32[]{:S(2)}) collective-permute-start(bf16[256,512]{1,0:T(8,128)(2,1)S(1)} %get-tuple-element.13), channel_id=1, source_target_pairs={{16,0},{17,1},{18,2},{19,3},{20,4},{21,5},{22,6},{23,7},{24,8},{25... | collective-permute-start | bytes 786440 | tf_op jit(solution)/shard_map/ppermute | solution.py:12
  191.8 34.6 %copy-start.17 = (bf16[256,512]{1,0:T(8,128)(2,1)}, bf16[256,512]{1,0:T(8,128)(2,1)S(1)}, u32[]{:S(2)}) copy-start(bf16[256,512]{1,0:T(8,128)(2,1)S(1)} %slice_select_fusion.1) | copy-start | bytes 786436
  194.0 79.5 %all-reduce.14.cloned.1.call-start = ((), (), s32[]{:S(2)}) async-start(), calls=%async_computation.8 | async-start | bytes 524288 | tf_op jit(solution)/shard_map/psum | solution.py:114
  228.3 8.5 %collective-permute-start.1 = (bf16[256,512]{1,0:T(8,128)(2,1)S(1)}, bf16[256,512]{1,0:T(8,128)(2,1)}, u32[]{:S(2)}, u32[]{:S(2)}) collective-permute-start(bf16[256,512]{1,0:T(8,128)(2,1)S(1)} %get-tuple-element.11), channel_id=1, source_target_pairs={{16,0},{17,1},{18,2},{19,3},{20,4},{21,5},{22,6},{23,7},{24,8},{25... | collective-permute-start | bytes 786440 | tf_op jit(solution)/shard_map/ppermute | solution.py:12
  241.0 79.5 %all-reduce.16.cloned.1.call-start = ((), (), s32[]{:S(2)}) async-start(), calls=%async_computation.9 | async-start | bytes 524288 | tf_op jit(solution)/shard_map/psum | solution.py:114
  275.4 8.7 %collective-permute-start.2 = (bf16[256,512]{1,0:T(8,128)(2,1)}, bf16[256,512]{1,0:T(8,128)(2,1)}, u32[]{:S(2)}, u32[]{:S(2)}) collective-permute-start(bf16[256,512]{1,0:T(8,128)(2,1)} %get-tuple-element.9), channel_id=1, source_target_pairs={{16,0},{17,1},{18,2},{19,3},{20,4},{21,5},{22,6},{23,7},{24,8},{25... | collective-permute-start | bytes 786440 | tf_op jit(solution)/shard_map/ppermute | solution.py:12
  276.7 9.2 %copy-start.31 = (bf16[1,512,512]{2,1,0:T(8,128)(2,1)S(1)}, bf16[1,512,512]{2,1,0:T(8,128)(2,1)}, u32[]{:S(2)}) copy-start(bf16[1,512,512]{2,1,0:T(8,128)(2,1)} %param.11) | copy-start | bytes 1572868
  277.0 9.3 %copy-start.25 = (f32[256,512]{1,0:T(8,128)}, f32[256,512]{1,0:T(8,128)S(1)}, u32[]{:S(2)}) copy-start(f32[256,512]{1,0:T(8,128)S(1)} %fusion.26) | copy-start | bytes 1572868
  288.1 79.5 %all-reduce.18.cloned.1.call-start = ((), (), s32[]{:S(2)}) async-start(), calls=%async_computation.10 | async-start | bytes 524288 | tf_op jit(solution)/shard_map/psum | solution.py:114
  322.5 8.7 %collective-permute-start.3 = (bf16[256,512]{1,0:T(8,128)(2,1)}, bf16[256,512]{1,0:T(8,128)(2,1)}, u32[]{:S(2)}, u32[]{:S(2)}) collective-permute-start(bf16[256,512]{1,0:T(8,128)(2,1)} %get-tuple-element.7), channel_id=1, source_target_pairs={{16,0},{17,1},{18,2},{19,3},{20,4},{21,5},{22,6},{23,7},{24,8},{25... | collective-permute-start | bytes 786440 | tf_op jit(solution)/shard_map/ppermute | solution.py:12
  324.0 9.0 %copy-start.32 = (bf16[1,512,512]{2,1,0:T(8,128)(2,1)S(1)}, bf16[1,512,512]{2,1,0:T(8,128)(2,1)}, u32[]{:S(2)}) copy-start(bf16[1,512,512]{2,1,0:T(8,128)(2,1)} %param.11) | copy-start | bytes 1572868
  324.3 9.1 %copy-start.26 = (f32[256,512]{1,0:T(8,128)}, f32[256,512]{1,0:T(8,128)S(1)}, u32[]{:S(2)}) copy-start(f32[256,512]{1,0:T(8,128)S(1)} %fusion.23) | copy-start | bytes 1572868
  335.2 62.0 %reduce-scatter.4.cloned.1.call-start = ((), (), s32[]{:S(2)}) async-start(), calls=%async_computation.4 | async-start | bytes 1310720 | tf_op jit(solution)/shard_map/reduce_scatter | solution.py:82
  339.2 81.2 %reduce-scatter.6.cloned.1.call-start = ((), (), s32[]{:S(2)}) async-start(), calls=%async_computation.12 | async-start | bytes 655360 | tf_op jit(solution)/shard_map/reduce_scatter | solution.py:128
  345.3 97.4 %reduce-scatter.8.cloned.1.call-start = ((), (), s32[]{:S(2)}) async-start(), calls=%async_computation.13 | async-start | bytes 655360 | tf_op jit(solution)/shard_map/reduce_scatter | solution.py:131
  350.5 132.9 %all-reduce.20.cloned.1.call-start = ((), (), s32[]{:S(2)}) async-start(), calls=%async_computation.11 | async-start | bytes 2097152 | tf_op jit(solution)/shard_map/psum | solution.py:17
  367.6 29.6 %copy-start.5 = (bf16[256,512]{1,0:T(8,128)(2,1)S(1)}, bf16[256,512]{1,0:T(8,128)(2,1)}, u32[]{:S(2)}) copy-start(bf16[256,512]{1,0:T(8,128)(2,1)} %param.7) | copy-start | bytes 786436
  (24 other events, 50.3 us)
Sparse Core Ops, SparseCore 0:
  10.4 30.6 all-gather.1
  90.8 50.3 all-reduce.7
  147.2 32.3 all-reduce.9
  194.1 32.2 all-reduce.11
  241.1 32.2 all-reduce.13
  288.2 32.2 all-reduce.15
  335.3 32.2 all-reduce.17
  369.9 27.2 reduce-scatter.3
  400.1 20.3 reduce-scatter.5
  422.5 20.0 reduce-scatter.7
  445.0 38.3 all-reduce.19
where the time goes:
time: 493 us; the launch traced here: 492 us
  waiting for transfers between devices  358 us (73%)
  other arithmetic  39.4 us (8%)
  blocking collectives  31 us (6%)
  matrix products  30.8 us (6%)
  between operations  15.1 us (3%)
  local copies, waits for them, and re-layouts  12.1 us (2%)
  starting transfers between devices  5.75 us (1%)
    psum x5, waiting for transfers between devices, body(): summed = lax.psum(unit_share.astype(jnp.bfloat16), 'mp').astype(jnp.float32)  147 us
    psum x1, waiting for transfers between devices, body(): text_unit_grad = lax.psum(text_share, 'mp')  49.2 us
    psum x1, waiting for transfers between devices, spread(): return lax.psum(kept, axis)  39.1 us
    all_gather x1, waiting for transfers between devices, body(): columns = lax.all_gather(image_low, 'dp', axis=0, tiled=True)  28.6 us
    ppermute x4, waiting for transfers between devices, shifted(): return lax.ppermute(block, axis, route)  27.7 us
    reduce_scatter x1, waiting for transfers between devices, body(): lax.psum_scatter((logit_mult * contract_rows(score_grad, text_low)).astyp...  25.4 us
    reduce_scatter x1, waiting for transfers between devices, body(): lax.psum_scatter(grad_second.astype(jnp.bfloat16), 'dp', scatter_dimensio...  20.6 us
    reduce_scatter x1, waiting for transfers between devices, body(): lax.psum_scatter(grad_first.astype(jnp.bfloat16), 'dp', scatter_dimension...  20.2 us
  transfers between devices with their start and end apart: 15, of which 15 were waited for; matrix products, arithmetic and copies ran while one was open for 6% of the time, Pallas kernels for 0%

commit v1 on v0

v1 whole, which is shorter than its diff:
```python
import jax
import jax.numpy as jnp
from jax import lax
from jax.experimental import pallas as pl
from jax.experimental.pallas import tpu as pltpu
from jax.sharding import PartitionSpec as P

MESH = pl.DeviceIdType.MESH
F32 = jnp.float32
BF16 = jnp.bfloat16
GELU = 1.702
LANES = 128


def unit_rows(values):
    wide = values.astype(F32)
    length = jnp.sqrt(jnp.sum(wide * wide, axis=1, keepdims=True) + 1.0)
    return (wide / length, length)


def unit_backward(unit, length, grad_unit):
    return (grad_unit - unit * jnp.sum(unit * grad_unit, axis=1, keepdims=True)) / length


def dot_nn(a, b):
    return lax.dot_general(a, b, (((1,), (0,)), ((), ())), preferred_element_type=F32)


def dot_nt(a, b):
    return lax.dot_general(a, b, (((1,), (1,)), ((), ())), preferred_element_type=F32)


def dot_tn(a, b):
    return lax.dot_general(a, b, (((0,), (0,)), ((), ())), preferred_element_type=F32)


def tile(index, size):
    return pl.ds(pl.multiple_of(index * size, size), size)


def make_kernel(n_sec, n_dp, n_mp):
    cores = 2 if n_mp % 2 == 0 else 1
    chips = n_mp // cores

    def kernel(
        text, image, scale_ref, hidden, w_in, w_out,
        image_out, input_out, first_out, second_out,
        text_low, cols, scores, sgrad, row_max, row_lse, row_st, row_rx, col_st, col_rx,
        wi_all, wo_all, t_tx, t_rx, t_own, g_all, g_acc, g_new, act_all, pre_all,
        w_tx, w_rx, i_tx, i_rx,
        gat_s, gat_r, fwd_s, fwd_r, cs_s, cs_r, rs_s, rs_r, wi_s, wi_r, wo_s, wo_r,
        t_s, t_r, g_s, g_r, x_s, x_r, in_s, in_r, ix_s, ix_r, w_s, w_r, im_s, im_r, io_s, io_r,
    ):
        s = lax.axis_index("section")
        d = lax.axis_index("dp")
        m = lax.axis_index("mp")
        last = n_sec - 1
        rows = text.shape[0]
        own = image.shape[0]
        half = own // n_sec
        quarter = rows // n_mp
        feats = text.shape[1]
        share = feats // n_dp
        width = feats // n_sec
        mult = scale_ref[0]
        core = lax.rem(m, cores)
        chip = m // cores

        def copy(src, dst, send, recv, where):
            return pltpu.make_async_remote_copy(
                src_ref=src, dst_ref=dst, send_sem=send, recv_sem=recv,
                device_id=where, device_id_type=MESH,
            )

        def others(mine, count):
            return [lax.rem(mine + k, count) for k in range(1, count)]

        def sources(mine, count):
            return [lax.rem(mine + count - k, count) for k in range(1, count)]

        barrier = pltpu.get_barrier_semaphore()
        for p in others(d, n_dp):
            pl.semaphore_signal(barrier, inc=1, device_id={"dp": p}, device_id_type=MESH)
        for p in others(m, n_mp):
            pl.semaphore_signal(barrier, inc=1, device_id={"mp": p}, device_id_type=MESH)
        for p in others(s, n_sec):
            pl.semaphore_signal(barrier, inc=1, device_id={"section": p}, device_id_type=MESH)

        own_unit, _ = unit_rows(image[...])
        cols[tile(d, own), :] = own_unit.astype(BF16)
        pl.semaphore_wait(barrier, n_dp + n_mp + n_sec - 3)

        def cut(block, sec):
            return cols.at[pl.ds(pl.multiple_of(block * own + sec * half, half), half), :]

        gathers = []
        for p in others(d, n_dp):
            c = copy(cut(d, s), cut(d, s), gat_s.at[p], gat_r.at[d], {"dp": p})
            c.start()
            gathers.append(c)

        class Spread:
            def __init__(self, slot, send, recv):
                self.slot, self.send, self.recv = slot, send, recv
                self.sent = []

            def push(self, index, to):
                c = copy(self.slot(index), self.slot(index), self.send.at[len(self.sent)],
                         self.recv.at[index], {"mp": to})
                c.start()
                self.sent.append(c)

            def arrived(self, index):
                copy(self.slot(index), self.slot(index), self.send.at[0],
                     self.recv.at[index], {"mp": lax.rem(m + 1, n_mp)}).wait_recv()

            def start(self):
                for q in others(chip, chips):
                    self.push(m, q * cores + core)
                for e in others(core, cores):
                    self.push(m, chip * cores + e)

            def relay(self):
                for q in sources(chip, chips):
                    index = q * cores + core
                    self.arrived(index)
                    for e in others(core, cores):
                        self.push(index, chip * cores + e)

            def finish(self):
                for e in sources(core, cores):
                    self.arrived(chip * cores + e)
                    for q in sources(chip, chips):
                        self.arrived(q * cores + e)

            def drain(self):
                for c in self.sent:
                    c.wait_send()

        wi_all[m] = w_in[...]
        wo_all[m] = w_out[...]
        wi_spread = Spread(lambda k: wi_all.at[k], wi_s, wi_r)
        wo_spread = Spread(lambda k: wo_all.at[k], wo_s, wo_r)
        wi_spread.start()
        wo_spread.start()

        @pl.loop(0, n_mp)
        def _(r):
            unit, _ = unit_rows(text[tile(r, quarter), :])
            text_low[tile(r, quarter), :] = unit.astype(BF16)

        row_max[...] = jnp.full(row_max.shape, -1e30, F32)

        def block_scores(p):
            piece = cols[tile(p, own), :]

            def chunk(r, peak):
                value = mult * dot_nt(text_low[tile(r, quarter), :], piece)
                scores[tile(r, quarter), tile(p, own)] = value
                best = row_max[tile(r, quarter), :]
                for k in range(0, own, LANES):
                    best = jnp.maximum(best, value[:, k : k + LANES])
                row_max[tile(r, quarter), :] = best
                return jnp.maximum(peak, jnp.max(value, axis=0, keepdims=True))

            peak = lax.fori_loop(0, n_mp, chunk, jnp.full((1, own), -1e30, F32))

            def total(r, acc):
                value = scores[tile(r, quarter), tile(p, own)]
                return acc + jnp.sum(jnp.exp(value - peak), axis=0, keepdims=True)

            acc = lax.fori_loop(0, n_mp, total, jnp.zeros((1, own), F32))
            col_st[pl.ds(p, 1), :] = peak
            col_st[pl.ds(n_dp + p, 1), :] = acc

        block_scores(d)
        forwards = []
        for k, p in enumerate(sources(d, n_dp)):
            copy(cut(p, s), cut(p, s), gat_s.at[p], gat_r.at[p], {"dp": p}).wait_recv()
            for t in others(s, n_sec):
                c = copy(cut(p, s), cut(p, s), fwd_s.at[t, p], fwd_r.at[s, p], {"section": t})
                c.start()
                forwards.append(c)
        for p in sources(d, n_dp):
            for t in sources(s, n_sec):
                copy(cut(p, t), cut(p, t), fwd_s.at[t, p], fwd_r.at[t, p],
                     {"section": t}).wait_recv()
            block_scores(p)

        col_rx[d] = col_st[...]
        col_sent = []
        for p in others(d, n_dp):
            c = copy(col_st, col_rx.at[d], cs_s.at[p], cs_r.at[d], {"dp": p})
            c.start()
            col_sent.append(c)

        for r in range(n_mp):
            part = pl.ds(r * quarter, quarter)
            peak = jnp.max(row_max[part, :], axis=1, keepdims=True)

            def total(p, acc):
                value = jnp.exp(scores[part, tile(p, own)] - peak)
                for k in range(0, own, LANES):
                    acc = acc + value[:, k : k + LANES]
                return acc

            acc = lax.fori_loop(0, n_dp, total, jnp.zeros((quarter, LANES), F32))
            acc = jnp.sum(acc, axis=1, keepdims=True)
            wide_peak = jnp.broadcast_to(peak, (quarter, LANES)).T
            wide_sum = jnp.broadcast_to(acc, (quarter, LANES)).T
            row_st[r : r + 1, :] = wide_peak[0:1, :]
            row_st[n_mp + r : n_mp + r + 1, :] = wide_sum[0:1, :]

        row_rx[m] = row_st[...]
        row_sent = []
        for p in others(m, n_mp):
            c = copy(row_st, row_rx.at[m], rs_s.at[p], rs_r.at[m], {"mp": p})
            c.start()
            row_sent.append(c)

        def merge(rx, count, n):
            peak = rx[0, 0:n, :]
            for k in range(1, count):
                peak = jnp.maximum(peak, rx[k, 0:n, :])
            acc = jnp.zeros(peak.shape, F32)
            for k in range(count):
                acc = acc + rx[k, n : 2 * n, :] * jnp.exp(rx[k, 0:n, :] - peak)
            return peak + jnp.log(acc)

        for p in sources(d, n_dp):
            copy(col_st, col_rx.at[p], cs_s.at[p], cs_r.at[p], {"dp": p}).wait_recv()
        col_lse = merge(col_rx, n_dp, n_dp)
        col_st_rows = [col_lse[k : k + 1, :] for k in range(n_dp)]
        for p in sources(m, n_mp):
            copy(row_st, row_rx.at[p], rs_s.at[p], rs_r.at[p], {"mp": p}).wait_recv()
        merged = merge(row_rx, n_mp, n_mp)
        for r in range(n_mp):
            row_lse[r] = jnp.broadcast_to(merged[r : r + 1, :], (LANES, quarter)).T

        def score_rows(r):
            line = row_lse[r]
            text_id = lax.broadcasted_iota(jnp.int32, (quarter, LANES), 0) + d * rows + r * quarter
            for p in range(n_dp):
                for k in range(0, own, LANES):
                    value = scores[tile(r, quarter), p * own + k : p * own + k + LANES]
                    both = jnp.exp(value - line) + jnp.exp(value - col_st_rows[p][:, k : k + LANES])
                    image_id = lax.broadcasted_iota(jnp.int32, (quarter, LANES), 1) + (
                        (p * n_mp + m) * own + k
                    )
                    out = 0.5 * both - jnp.where(text_id == image_id, 1.0, 0.0)
                    sgrad[tile(r, quarter), p * own + k : p * own + k + LANES] = out.astype(BF16)

        @pl.loop(0, n_mp)
        def _(k):
            r = lax.rem(m + 1 + k, n_mp)
            score_rows(r)

            @pl.when(s == last)
            def _():
                value = dot_nn(sgrad[tile(r, quarter), :], cols[...])

                @pl.when(k < n_mp - 1)
                def _():
                    t_tx[r] = value.astype(BF16)
                    copy(t_tx.at[r], t_rx.at[m], t_s.at[r], t_r.at[m], {"mp": r}).start()

                @pl.when(k == n_mp - 1)
                def _():
                    t_own[...] = value

        def image_part(p):
            at = pl.ds(pl.multiple_of(p * own + s * half, half), half)
            return dot_tn(sgrad[:, at], text_low[...])

        image_sent = []
        for p in others(d, n_dp):
            i_tx[p] = image_part(p).astype(BF16)
            c = copy(i_tx.at[p], i_rx.at[d], im_s.at[p], im_r.at[d], {"dp": p})
            c.start()
            image_sent.append(c)

        wi_spread.relay()
        wo_spread.relay()

        mine = tile(m, quarter)

        @pl.when(s == last)
        def _():
            total = t_own[...]
            for p in sources(m, n_mp):
                copy(t_tx.at[p], t_rx.at[p], t_s.at[p], t_r.at[p], {"mp": p}).wait_recv()
                total = total + t_rx[p].astype(F32)
            unit, length = unit_rows(text[mine, :])
            g_all[m] = unit_backward(unit, length, mult * total).astype(BF16)

        wi_spread.finish()
        wo_spread.finish()

        @pl.when(s != last)
        def _():
            copy(g_new, g_all.at[m], x_s, x_r, {"section": s + 1}).wait_recv()

        g_spread = Spread(lambda k: g_all.at[k], g_s, g_r)
        g_spread.start()

        def slopes(pre, back):
            sigm = 1.0 / (1.0 + jnp.exp(-GELU * pre))
            grad = back * (sigm + GELU * pre * sigm * (1.0 - sigm))
            return (pre * sigm).astype(BF16), grad.astype(BF16)

        g_acc[...] = g_all[m].astype(F32)

        @pl.loop(0, n_mp)
        def _(j):
            pre = dot_nn(hidden[mine, :], wi_all[j])
            back = dot_nt(g_all[m], wo_all[j])
            _, grad = slopes(pre, back)
            g_acc[...] += dot_nt(grad, wi_all[j])

        g_new[...] = g_acc[...].astype(BF16)

        @pl.when(s > 0)
        def _():
            copy(g_new, g_all.at[m], x_s, x_r, {"section": s - 1}).start()

        def slab(k):
            return input_out.at[tile(k, quarter), :]

        def final(t):
            return copy(g_new.at[:, t * width : (t + 1) * width], slab(m), ix_s.at[t], ix_r,
                        {"section": t})

        @pl.when(s == 0)
        def _():
            for t in range(1, n_sec):
                final(t).start()
            input_out[mine, :] = g_new[:, 0:width]

        g_spread.relay()
        g_spread.finish()
        in_spread = Spread(slab, in_s, in_r)

        @pl.loop(0, n_mp)
        def _(r):
            pre = dot_nn(hidden[tile(r, quarter), :], w_in[...])
            back = dot_nt(g_all[r], w_out[...])
            act, grad = slopes(pre, back)
            act_all[tile(r, quarter), :] = act
            pre_all[tile(r, quarter), :] = grad

        g_rows = g_all[...].reshape(rows, feats)
        grad_second = dot_tn(g_rows, act_all[...])
        for p in range(n_dp):
            w_tx[p, 1] = grad_second[p * share : (p + 1) * share, :].astype(BF16)
        weight_sent = []

        def send_weights(which):
            for p in others(d, n_dp):
                c = copy(w_tx.at[p, which], w_rx.at[d, which], w_s.at[which, p],
                         w_r.at[which, d], {"dp": p})
                c.start()
                weight_sent.append(c)

        send_weights(1)
        grad_first = dot_tn(hidden[...], pre_all[...])
        for p in range(n_dp):
            w_tx[p, 0] = grad_first[p * share : (p + 1) * share, :].astype(BF16)
        send_weights(0)

        @pl.when(s != 0)
        def _():
            copy(g_new.at[:, 0:width], slab(m), ix_s.at[0], ix_r, {"section": 0}).wait_recv()

        in_spread.start()

        image_half = pl.ds(pl.multiple_of(s * half, half), half)
        total = image_part(d)
        for p in sources(d, n_dp):
            copy(i_tx.at[p], i_rx.at[p], im_s.at[p], im_r.at[p], {"dp": p}).wait_recv()
            total = total + i_rx[p].astype(F32)
        unit, length = unit_rows(image[image_half, :])
        image_out[image_half, :] = unit_backward(unit, length, mult * total).astype(BF16)
        out_sent = []
        for t in others(s, n_sec):
            c = copy(image_out.at[image_half, :], image_out.at[image_half, :],
                     io_s.at[t], io_r.at[s], {"section": t})
            c.start()
            out_sent.append(c)

        in_spread.relay()
        in_spread.finish()

        for which, out in ((1, second_out), (0, first_out)):
            total = w_tx[d, which].astype(F32)
            for p in sources(d, n_dp):
                copy(w_tx.at[p, which], w_rx.at[p, which], w_s.at[which, p],
                     w_r.at[which, p], {"dp": p}).wait_recv()
                total = total + w_rx[p, which].astype(F32)
            out[...] = total

        for t in sources(s, n_sec):
            part = image_out.at[pl.ds(pl.multiple_of(t * half, half), half), :]
            copy(part, part, io_s.at[t], io_r.at[t], {"section": t}).wait_recv()

        for c in gathers + forwards + col_sent + row_sent + image_sent + weight_sent + out_sent:
            c.wait_send()
        for spread in (wi_spread, wo_spread, g_spread, in_spread):
            spread.drain()

        @pl.when(s == last)
        def _():
            for p in others(m, n_mp):
                copy(t_tx.at[p], t_rx.at[m], t_s.at[p], t_r.at[m], {"mp": p}).wait_send()

        @pl.when(s > 0)
        def _():
            copy(g_new, g_all.at[m], x_s, x_r, {"section": s - 1}).wait_send()

        @pl.when(s == 0)
        def _():
            for t in range(1, n_sec):
                final(t).wait_send()

    return kernel


def solution(mesh):
    n_sec, n_dp, n_mp = mesh.shape["section"], mesh.shape["dp"], mesh.shape["mp"]

    def body(text, image, scale, hidden, w_in, w_out):
        rows, feats = text.shape
        own = image.shape[0]
        hid = w_in.shape[2]
        quarter, half, share = rows // n_mp, own // n_sec, feats // n_dp
        columns = own * n_dp
        dma = pltpu.SemaphoreType.DMA
        vmem = pl.BlockSpec(memory_space=pltpu.VMEM)
        out = pl.pallas_call(
            make_kernel(n_sec, n_dp, n_mp),
            out_shape=(
                jax.ShapeDtypeStruct((own, feats), BF16),
                jax.ShapeDtypeStruct((rows, feats // n_sec), BF16),
                jax.ShapeDtypeStruct((share, hid), F32),
                jax.ShapeDtypeStruct((share, hid), F32),
            ),
            in_specs=[vmem, vmem, pl.BlockSpec(memory_space=pltpu.SMEM), vmem, vmem, vmem],
            out_specs=(vmem,) * 4,
            scratch_shapes=[
                pltpu.VMEM((rows, feats), BF16),
                pltpu.VMEM((columns, feats), BF16),
                pltpu.VMEM((rows, columns), F32),
                pltpu.VMEM((rows, columns), BF16),
                pltpu.VMEM((rows, LANES), F32),
                pltpu.VMEM((n_mp, quarter, LANES), F32),
                pltpu.VMEM((2 * n_mp, quarter), F32),
                pltpu.VMEM((n_mp, 2 * n_mp, quarter), F32),
                pltpu.VMEM((2 * n_dp, own), F32),
                pltpu.VMEM((n_dp, 2 * n_dp, own), F32),
                pltpu.VMEM((n_mp, feats, hid), BF16),
                pltpu.VMEM((n_mp, hid, feats), BF16),
                pltpu.VMEM((n_mp, quarter, feats), BF16),
                pltpu.VMEM((n_mp, quarter, feats), BF16),
                pltpu.VMEM((quarter, feats), F32),
                pltpu.VMEM((n_mp, quarter, feats), BF16),
                pltpu.VMEM((quarter, feats), F32),
                pltpu.VMEM((quarter, feats), BF16),
                pltpu.VMEM((rows, hid), BF16),
                pltpu.VMEM((rows, hid), BF16),
                pltpu.VMEM((n_dp, 2, share, hid), BF16),
                pltpu.VMEM((n_dp, 2, share, hid), BF16),
                pltpu.VMEM((n_dp, half, feats), BF16),
                pltpu.VMEM((n_dp, half, feats), BF16),
                dma((n_dp,)), dma((n_dp,)),
                dma((n_sec, n_dp)), dma((n_sec, n_dp)),
                dma((n_dp,)), dma((n_dp,)),
                dma((n_mp,)), dma((n_mp,)),
                dma((2 * n_mp,)), dma((n_mp,)),
                dma((2 * n_mp,)), dma((n_mp,)),
                dma((n_mp,)), dma((n_mp,)),
                dma((2 * n_mp,)), dma((n_mp,)),
                dma, dma,
                dma((2 * n_mp,)), dma((n_mp,)),
                dma((n_sec,)), dma,
                dma((2, n_dp)), dma((2, n_dp)),
                dma((n_dp,)), dma((n_dp,)),
                dma((n_sec,)), dma((n_sec,)),
            ],
            compiler_params=pltpu.CompilerParams(
                collective_id=0, has_side_effects=True, vmem_limit_bytes=63000000
            ),
        )(text, image, scale, hidden[0], w_in[0], w_out[0])
        image_grad, input_grad, first, second = out
        return (image_grad, input_grad, first[None], second[None])

    return jax.shard_map(
        body,
        mesh=mesh,
        in_specs=(
            P("dp", None),
            P(("dp", "mp"), None),
            P(),
            P("section", "dp", None),
            P("section", None, "mp"),
            P("section", "mp", None),
        ),
        out_specs=(
            P(("dp", "mp"), None),
            P("dp", "section"),
            P("section", "dp", "mp"),
            P("section", "dp", "mp"),
        ),
        check_vma=False,
    )
```

time: 493 us -> 92.7 us (0.19)
  waiting for transfers between devices: 358 us -> 0 us
  Pallas kernels: 0 us -> 86.6 us
  other arithmetic: 39.4 us -> 0 us
  blocking collectives: 31 us -> 0 us
  matrix products: 30.8 us -> 0 us
  between operations: 15.1 us -> 1.3 us
  local copies, waits for them, and re-layouts: 12.1 us -> 4.57 us
  starting transfers between devices: 5.75 us -> 0 us
    psum x7 -> x0, waiting for transfers between devices: 235 us -> none  [the longest x5 147 us: body(): summed = lax.psum(unit_share.astype(jnp.bfloat16), 'mp').astype(jnp.float32)]
    pallas_call x0 -> x1, Pallas kernels: none -> 86.6 us  [body(): pl.pallas_call(make_kernel(n_sec, n_dp, n_mp), out_shape=(jax.ShapeDtypeS...]
    reduce_scatter x3 -> x0, waiting for transfers between devices: 66.2 us -> none  [the longest x1 25.4 us: body(): lax.psum_scatter((logit_mult * contract_rows(score_grad, text_low)).astyp...]
    dot_general x28 -> x0, matrix products: 30.8 us -> none  [the longest x11 14 us: contract_rows(): lax.dot_general(left_side, right_side, (((0,), (0,)), ((), ())), preferre...]
    all_gather x1 -> x0, waiting for transfers between devices: 28.6 us -> none  [body(): columns = lax.all_gather(image_low, 'dp', axis=0, tiled=True)]
    ppermute x4 -> x0, waiting for transfers between devices: 27.7 us -> none  [shifted(): return lax.ppermute(block, axis, route)]
    pmax x2 -> x0, blocking collectives: 17 us -> none  [the longest x1 10.9 us: body(): column_peak = lax.pmax(jnp.max(scores, axis=0), 'dp')]
    select_n x10 -> x0, other arithmetic: 15.9 us -> none  [the longest x5 9.48 us: body(): finished = jnp.where(jnp.logical_and(active, is_first), updated, finished)]
  transfers between devices with their start and end apart: 15 -> 0, of which waited for: 15 -> 0; matrix products, arithmetic and copies ran while one was open for 6% -> 0% of each run, Pallas kernels for 0% -> 0%
where the time goes in v1:
time: 92.7 us; the launch traced here: 92.5 us
  Pallas kernels  86.6 us (93%)
  local copies, waits for them, and re-layouts  4.57 us (5%)
  between operations  1.3 us (1%)
    pallas_call x1, Pallas kernels, body(): pl.pallas_call(make_kernel(n_sec, n_dp, n_mp), out_shape=(jax.ShapeDtypeS...  86.6 us
    unnamed x10, local copies, waits for them, and re-layouts  4.57 us

profile of v1, /device:TPU:0, one launch (start us, length us, event | category | flops | bytes accessed | tf_op | source)
XLA Modules:
  0.0 92.5 jit_solution(4735918846649673005)
XLA Ops:
  1.3 86.6 %shard_map.93 = (bf16[256,512]{1,0:T(8,128)(2,1)}, bf16[1024,256]{1,0:T(8,128)(2,1)}, f32[128,512]{1,0:T(8,128)}, f32[128,512]{1,0:T(8,128)}) custom-call(bf16[1024,512]{1,0:T(8,128)(2,1)} %text.1, bf16[256,512]{1,0:T(8,128)(2,1)} %image.1, f32[1]{0:T(128)S(6)} %copy.14.scale_ref, bf16[1024,512]{1,0:T(8,128)(2,1)} %bitcast.5, bf16[512,512]{1,0:T(8,128)(2,1)} %bitcast.6, ...), custom_call_target="tpu_custom_call" | custom-call | tf_op jit(solution)/shard_map/pallas_call | solution.py:438
  87.9 0.0 copy-start
  87.9 1.7 %copy.15 = bf16[256,512]{1,0:T(8,128)(2,1)} copy(bf16[256,512]{1,0:T(8,128)(2,1)} %get-tuple-element.16) | data formatting | bytes 524288
  89.6 0.0 copy-done
  89.6 0.0 copy-start.2
  89.6 0.8 copy.16
  90.4 0.3 copy-done.2
  90.7 0.0 copy-start.1
  90.7 0.7 copy.17
  91.4 0.3 copy-done.1
  91.8 0.7 copy.18
Async XLA Ops:
  87.9 1.7 %copy-start = (bf16[1024,256]{1,0:T(8,128)(2,1)S(1)}, bf16[1024,256]{1,0:T(8,128)(2,1)}, u32[]{:S(2)}) copy-start(bf16[1024,256]{1,0:T(8,128)(2,1)} %get-tuple-element.17) | copy-start | bytes 1572868
  89.6 1.1 %copy-start.2 = (f32[128,512]{1,0:T(8,128)S(1)}, f32[128,512]{1,0:T(8,128)}, u32[]{:S(2)}) copy-start(f32[128,512]{1,0:T(8,128)} %get-tuple-element.10) | copy-start | bytes 786436
  90.7 1.0 %copy-start.1 = (f32[128,512]{1,0:T(8,128)S(1)}, f32[128,512]{1,0:T(8,128)}, u32[]{:S(2)}) copy-start(f32[128,512]{1,0:T(8,128)} %get-tuple-element.11) | copy-start | bytes 786436

commit v2 on v1

--- a/solution.py
+++ b/solution.py
@@ -10,6 +10,7 @@
 BF16 = jnp.bfloat16
 GELU = 1.702
 LANES = 128
+PIECES = 2
 
 
 def unit_rows(values):
@@ -59,6 +60,7 @@
         own = image.shape[0]
         half = own // n_sec
         quarter = rows // n_mp
+        step = quarter // PIECES
         feats = text.shape[1]
         share = feats // n_dp
         width = feats // n_sec
@@ -105,14 +107,14 @@
                 self.sent = []
 
             def push(self, index, to):
-                c = copy(self.slot(index), self.slot(index), self.send.at[len(self.sent)],
-                         self.recv.at[index], {"mp": to})
+                c = copy(self.slot(index), self.slot(index), self.send(len(self.sent)),
+                         self.recv(index), {"mp": to})
                 c.start()
                 self.sent.append(c)
 
             def arrived(self, index):
-                copy(self.slot(index), self.slot(index), self.send.at[0],
-                     self.recv.at[index], {"mp": lax.rem(m + 1, n_mp)}).wait_recv()
+                copy(self.slot(index), self.slot(index), self.send(0),
+                     self.recv(index), {"mp": lax.rem(m + 1, n_mp)}).wait_recv()
 
             def start(self):
                 for q in others(chip, chips):
@@ -139,8 +141,8 @@
 
         wi_all[m] = w_in[...]
         wo_all[m] = w_out[...]
-        wi_spread = Spread(lambda k: wi_all.at[k], wi_s, wi_r)
-        wo_spread = Spread(lambda k: wo_all.at[k], wo_s, wo_r)
+        wi_spread = Spread(lambda k: wi_all.at[k], lambda k: wi_s.at[k], lambda k: wi_r.at[k])
+        wo_spread = Spread(lambda k: wo_all.at[k], lambda k: wo_s.at[k], lambda k: wo_r.at[k])
         wi_spread.start()
         wo_spread.start()
 
@@ -252,7 +254,8 @@
 
         @pl.loop(0, n_mp)
         def _(k):
-            r = lax.rem(m + 1 + k, n_mp)
+            to_chip = lax.rem(chip + 1 + k // cores, chips)
+            r = to_chip * cores + lax.rem(core + 1 + lax.rem(k, cores), cores)
             score_rows(r)
 
             @pl.when(s == last)
@@ -296,57 +299,81 @@
         wi_spread.finish()
         wo_spread.finish()
 
-        @pl.when(s != last)
-        def _():
-            copy(g_new, g_all.at[m], x_s, x_r, {"section": s + 1}).wait_recv()
-
-        g_spread = Spread(lambda k: g_all.at[k], g_s, g_r)
-        g_spread.start()
-
         def slopes(pre, back):
             sigm = 1.0 / (1.0 + jnp.exp(-GELU * pre))
             grad = back * (sigm + GELU * pre * sigm * (1.0 - sigm))
             return (pre * sigm).astype(BF16), grad.astype(BF16)
 
-        g_acc[...] = g_all[m].astype(F32)
-
-        @pl.loop(0, n_mp)
-        def _(j):
-            pre = dot_nn(hidden[mine, :], wi_all[j])
-            back = dot_nt(g_all[m], wo_all[j])
-            _, grad = slopes(pre, back)
-            g_acc[...] += dot_nt(grad, wi_all[j])
-
-        g_new[...] = g_acc[...].astype(BF16)
-
-        @pl.when(s > 0)
-        def _():
-            copy(g_new, g_all.at[m], x_s, x_r, {"section": s - 1}).start()
-
         def slab(k):
             return input_out.at[tile(k, quarter), :]
 
-        def final(t):
-            return copy(g_new.at[:, t * width : (t + 1) * width], slab(m), ix_s.at[t], ix_r,
-                        {"section": t})
+        def final(t, piece):
+            part = pl.ds(piece * step, step)
+            return copy(g_new.at[part, t * width : (t + 1) * width], slab(m).at[part, :],
+                        ix_s.at[t, piece], ix_r.at[piece], {"section": t})
+
+        def hop(piece, to):
+            part = pl.ds(piece * step, step)
+            return copy(g_new.at[part, :], g_all.at[m, part, :], x_s.at[piece], x_r.at[piece],
+                        {"section": to})
+
+        g_spreads = []
+        for piece in range(PIECES):
+            part = pl.ds(piece * step, step)
+
+            @pl.when(s != last)
+            def _():
+                hop(piece, s + 1).wait_recv()
+
+            spread = Spread(lambda k, part=part: g_all.at[k, part, :],
+                            lambda k, piece=piece: g_s.at[piece, k],
+                            lambda k, piece=piece: g_r.at[piece, k])
+            spread.start()
+            g_spreads.append(spread)
+            g_acc[part, :] = g_all[m, part, :].astype(F32)
+            rows_now = hidden[pl.ds(pl.multiple_of(m * quarter + piece * step, step), step), :]
+
+            @pl.loop(0, n_mp)
+            def _(j):
+                pre = dot_nn(rows_now, wi_all[j])
+                back = dot_nt(g_all[m, part, :], wo_all[j])
+                _, grad = slopes(pre, back)
+                g_acc[part, :] += dot_nt(grad, wi_all[j])
+
+            g_new[part, :] = g_acc[part, :].astype(BF16)
+
+            @pl.when(s > 0)
+            def _():
+                hop(piece, s - 1).start()
+
+            @pl.when(s == 0)
+            def _():
+                for t in range(1, n_sec):
+                    final(t, piece).start()
 
         @pl.when(s == 0)
         def _():
-            for t in range(1, n_sec):
-                final(t).start()
             input_out[mine, :] = g_new[:, 0:width]
 
-        g_spread.relay()
-        g_spread.finish()
-        in_spread = Spread(slab, in_s, in_r)
-
-        @pl.loop(0, n_mp)
-        def _(r):
+        for spread in g_spreads:
+            spread.relay()
+        in_spread = Spread(slab, lambda k: in_s.at[k], lambda k: in_r.at[k])
+
+        def weight_rows(r):
             pre = dot_nn(hidden[tile(r, quarter), :], w_in[...])
             back = dot_nt(g_all[r], w_out[...])
             act, grad = slopes(pre, back)
             act_all[tile(r, quarter), :] = act
             pre_all[tile(r, quarter), :] = grad
+
+        weight_rows(m)
+        for q in sources(chip, chips):
+            weight_rows(q * cores + core)
+        for e in sources(core, cores):
+            for index in [chip * cores + e] + [q * cores + e for q in sources(chip, chips)]:
+                for spread in g_spreads:
+                    spread.arrived(index)
+                weight_rows(index)
 
         g_rows = g_all[...].reshape(rows, feats)
         grad_second = dot_tn(g_rows, act_all[...])
@@ -369,7 +396,8 @@
 
         @pl.when(s != 0)
         def _():
-            copy(g_new.at[:, 0:width], slab(m), ix_s.at[0], ix_r, {"section": 0}).wait_recv()
+            for piece in range(PIECES):
+                final(0, piece).wait_recv()
 
         in_spread.start()
 
@@ -404,7 +432,7 @@
 
         for c in gathers + forwards + col_sent + row_sent + image_sent + weight_sent + out_sent:
             c.wait_send()
-        for spread in (wi_spread, wo_spread, g_spread, in_spread):
+        for spread in (wi_spread, wo_spread, *g_spreads, in_spread):
             spread.drain()
 
         @pl.when(s == last)
@@ -414,12 +442,14 @@
 
         @pl.when(s > 0)
         def _():
-            copy(g_new, g_all.at[m], x_s, x_r, {"section": s - 1}).wait_send()
+            for piece in range(PIECES):
+                hop(piece, s - 1).wait_send()
 
         @pl.when(s == 0)
         def _():
             for t in range(1, n_sec):
-                final(t).wait_send()
+                for piece in range(PIECES):
+                    final(t, piece).wait_send()
 
     return kernel
 
@@ -477,10 +507,10 @@
                 dma((2 * n_mp,)), dma((n_mp,)),
                 dma((2 * n_mp,)), dma((n_mp,)),
                 dma((n_mp,)), dma((n_mp,)),
+                dma((PIECES, 2 * n_mp)), dma((PIECES, n_mp)),
+                dma((PIECES,)), dma((PIECES,)),
                 dma((2 * n_mp,)), dma((n_mp,)),
-                dma, dma,
-                dma((2 * n_mp,)), dma((n_mp,)),
-                dma((n_sec,)), dma,
+                dma((n_sec, PIECES)), dma((PIECES,)),
                 dma((2, n_dp)), dma((2, n_dp)),
                 dma((n_dp,)), dma((n_dp,)),
                 dma((n_sec,)), dma((n_sec,)),

time: 92.7 us -> 93.5 us (level)
  no operation moved by 1% of the time
where the time goes in v2:
time: 93.5 us; the launch traced here: 93.3 us
  Pallas kernels  87.4 us (93%)
  local copies, waits for them, and re-layouts  4.57 us (5%)
  between operations  1.3 us (1%)
    pallas_call x1, Pallas kernels, body(): pl.pallas_call(make_kernel(n_sec, n_dp, n_mp), out_shape=(jax.ShapeDtypeS...  87.4 us
    unnamed x10, local copies, waits for them, and re-layouts  4.57 us

profile of v2, /device:TPU:0, one launch (start us, length us, event | category | flops | bytes accessed | tf_op | source)
XLA Modules:
  0.0 93.3 jit_solution(13293046287344019246)
XLA Ops:
  1.3 87.4 %shard_map.93 = (bf16[256,512]{1,0:T(8,128)(2,1)}, bf16[1024,256]{1,0:T(8,128)(2,1)}, f32[128,512]{1,0:T(8,128)}, f32[128,512]{1,0:T(8,128)}) custom-call(bf16[1024,512]{1,0:T(8,128)(2,1)} %text.1, bf16[256,512]{1,0:T(8,128)(2,1)} %image.1, f32[1]{0:T(128)S(6)} %copy.14.scale_ref, bf16[1024,512]{1,0:T(8,128)(2,1)} %bitcast.5, bf16[512,512]{1,0:T(8,128)(2,1)} %bitcast.6, ...), custom_call_target="tpu_custom_call" | custom-call | tf_op jit(solution)/shard_map/pallas_call | solution.py:468
  88.7 0.0 copy-start
  88.7 1.7 %copy.15 = bf16[256,512]{1,0:T(8,128)(2,1)} copy(bf16[256,512]{1,0:T(8,128)(2,1)} %get-tuple-element.16) | data formatting | bytes 524288
  90.4 0.0 copy-done
  90.4 0.0 copy-start.2
  90.4 0.8 copy.16
  91.2 0.3 copy-done.2
  91.5 0.0 copy-start.1
  91.5 0.7 copy.17
  92.2 0.3 copy-done.1
  92.6 0.7 copy.18
Async XLA Ops:
  88.7 1.7 %copy-start = (bf16[1024,256]{1,0:T(8,128)(2,1)S(1)}, bf16[1024,256]{1,0:T(8,128)(2,1)}, u32[]{:S(2)}) copy-start(bf16[1024,256]{1,0:T(8,128)(2,1)} %get-tuple-element.17) | copy-start | bytes 1572868
  90.4 1.1 %copy-start.2 = (f32[128,512]{1,0:T(8,128)S(1)}, f32[128,512]{1,0:T(8,128)}, u32[]{:S(2)}) copy-start(f32[128,512]{1,0:T(8,128)} %get-tuple-element.10) | copy-start | bytes 786436
  91.5 1.0 %copy-start.1 = (f32[128,512]{1,0:T(8,128)S(1)}, f32[128,512]{1,0:T(8,128)}, u32[]{:S(2)}) copy-start(f32[128,512]{1,0:T(8,128)} %get-tuple-element.11) | copy-start | bytes 786436
